TPU v7x, 32 devices: a whole 2x2x4 slice. The times are simulated.
32 devices in a mesh: section: 2 (over x), blk: 8 (over z, y), head: 2 (over core).
Axes of the slice: x: 2, y: 2, z: 4, core: 2. Of those that a mesh axis runs over, the one named last changes fastest.
Arguments:
- hidden_in: bfloat16 [4, 64, 1536], P(None, 'blk', 'head'), may hold values from -6 to 6
- w_qkv: bfloat16 [2, 1536, 3, 1536], P('section', 'blk', None, 'head'), may hold values from -0.15625 to 0.15625
- norm_gain: float32 [2, 1536], P('section'), may hold values from 0.5 to 1.5
- qk_gain: float32 [2, 2, 128], P('section'), may hold values from 1 to 2
- text_states: bfloat16 [2, 256, 1536], P('section'), may hold values from -6 to 6
- text_len: int32 [1], replicated, may hold values from 64 to 256
- patch_len: int32 [4], replicated, may hold values from 32 to 64
- stale_flags: int32 [4, 2], replicated, may hold values from 0 to 1, as said below
- stale_kv: bfloat16 [2, 2, 4, 64, 1536], P('section', None, None, 'blk', 'head'), may hold values from -6 to 6
Outputs:
- hidden_out: bfloat16 [2, 4, 64, 1536], P('section', None, 'blk', 'head')
- new_cache: bfloat16 [2, 2, 4, 64, 1536], P('section', None, None, 'blk', 'head')
Inputs may be any that keep to these rules, and one draw needn't show every extreme that they name: `stale_flags`: 1 means that the micro-batch uses the previous step's keys and values at that layer, 0 that it uses its fresh ones; every layer has at least one micro-batch flagged 1 and at least one flagged 0.
All inputs are finite; a program needn't handle non-finite values.
Results may differ from a plain program's by a relative error of at most 0.02.
Values may be sent and summed in bfloat16 or wider, within the bound.
A program may use at most 64 MiB of HBM per device.

v0:
```python
import jax
import jax.numpy as jnp
from jax import lax
from jax.sharding import PartitionSpec as P


def from_behind(value, axis, steps):
    count = lax.axis_size(axis)
    first, last = (max(0, -steps), min(count, count - steps))
    return lax.ppermute(value, axis, [(source, source + steps) for source in range(first, last)])


def norm_rows(values, row_gain):
    return values * lax.rsqrt(jnp.mean(values * values, axis=-1, keepdims=True) + 1e-06) * row_gain


def shards(
    hidden_in, w_qkv, norm_gain, qk_gain, text_states, text_len, patch_len, stale_flags, stale_kv
):
    n_section = lax.axis_size("section")
    section_idx = lax.axis_index("section")
    micro_count, tok_rows, half_width = hidden_in.shape
    head_dim = qk_gain.shape[2]
    heads_here = half_width // head_dim
    score_scale = head_dim ** (-0.5)
    weights = lax.all_gather(w_qkv[0], "blk", axis=0, tiled=True)
    row_gain = norm_gain[0]
    query_gain = qk_gain[0, 0]
    key_gain = qk_gain[0, 1]
    text_all = text_states[0]
    text_count = text_all.shape[0]
    text_normed = norm_rows(text_all.astype(jnp.float32), row_gain).astype(jnp.bfloat16)
    text_kv = jnp.einsum(
        "td,dch->tch", text_normed, weights[:, 1:], preferred_element_type=jnp.float32
    ).astype(jnp.bfloat16)
    text_keys = norm_rows(
        text_kv[:, 0].astype(jnp.float32).reshape(text_count, heads_here, head_dim), key_gain
    ).astype(jnp.bfloat16)
    text_values = text_kv[:, 1].reshape(text_count, heads_here, head_dim)
    text_mask = jnp.arange(text_count) < text_len[0]
    col_offset = lax.axis_index("head") * half_width

    def attend(queries, key_rows, value_rows, key_mask, totals):
        scores = (
            jnp.einsum("qhd,khd->hqk", queries, key_rows, preferred_element_type=jnp.float32)
            * score_scale
        )
        probs = jnp.where(key_mask[None, None, :], jnp.exp(scores), 0.0)
        numerator = totals[0] + jnp.einsum(
            "hqk,khd->qhd",
            probs.astype(jnp.bfloat16),
            value_rows,
            preferred_element_type=jnp.float32,
        )
        return (numerator, totals[1] + jnp.sum(probs, axis=2))

    whole_input = lax.all_gather(hidden_in, "head", axis=2, tiled=True)
    inflow_init = jnp.zeros((tok_rows, 2 * half_width), jnp.bfloat16)
    hidden_init = jnp.zeros((micro_count, tok_rows, half_width), jnp.bfloat16)
    cache_init = jnp.zeros((2, micro_count, tok_rows, half_width), jnp.bfloat16)

    def advance(tick, carried):
        inflow, hidden_acc, cache_acc = carried
        micro_at = tick - section_idx
        is_active = (micro_at >= 0) & (micro_at < micro_count)
        micro_at = jnp.clip(micro_at, 0, micro_count - 1)
        state_rows = jnp.where(
            section_idx == 0,
            lax.dynamic_index_in_dim(whole_input, micro_at, 0, keepdims=False),
            inflow,
        )
        state_float = state_rows.astype(jnp.float32)
        normed = norm_rows(state_float, row_gain).astype(jnp.bfloat16)
        projected = jnp.einsum("td,dch->tch", normed, weights, preferred_element_type=jnp.float32)
        fresh_kv = jnp.moveaxis(projected[:, 1:], 1, 0).astype(jnp.bfloat16)
        use_stale = lax.dynamic_slice(stale_flags, (micro_at, section_idx), (1, 1))[0, 0]
        stale_here = lax.dynamic_index_in_dim(stale_kv[0], micro_at, 1, keepdims=False)
        kept_kv = jnp.where(use_stale == 1, stale_here, fresh_kv)
        key_rows = norm_rows(
            kept_kv[0].astype(jnp.float32).reshape(tok_rows, heads_here, head_dim), key_gain
        ).astype(jnp.bfloat16)
        value_rows = kept_kv[1].reshape(tok_rows, heads_here, head_dim)
        queries = norm_rows(
            projected[:, 0].reshape(tok_rows, heads_here, head_dim), query_gain
        ).astype(jnp.bfloat16)
        patch_limit = lax.dynamic_index_in_dim(patch_len, micro_at, 0, keepdims=False)
        zero_num = jnp.zeros((tok_rows, heads_here, head_dim), jnp.float32)
        zero_den = jnp.zeros((heads_here, tok_rows), jnp.float32)
        text_totals = attend(queries, text_keys, text_values, text_mask, (zero_num, zero_den))
        piece_keys = lax.all_gather(key_rows, "blk", axis=0, tiled=True)
        piece_values = lax.all_gather(value_rows, "blk", axis=0, tiled=True)
        key_mask = jnp.arange(piece_keys.shape[0]) < patch_limit
        numerator, denominator = attend(queries, piece_keys, piece_values, key_mask, text_totals)
        attended = (numerator / jnp.transpose(denominator)[:, :, None]).reshape(
            tok_rows, half_width
        )
        own_rows = lax.dynamic_slice_in_dim(state_float, col_offset, half_width, 1)
        new_half = (own_rows + attended).astype(jnp.bfloat16)
        hidden_acc = jnp.where(
            is_active,
            lax.dynamic_update_index_in_dim(hidden_acc, new_half, micro_at, 0),
            hidden_acc,
        )
        cache_acc = jnp.where(
            is_active, lax.dynamic_update_index_in_dim(cache_acc, fresh_kv, micro_at, 1), cache_acc
        )
        whole_next = lax.all_gather(new_half, "head", axis=1, tiled=True)
        inflow = from_behind(whole_next, "section", 1)
        return (inflow, hidden_acc, cache_acc)

    finished = lax.fori_loop(
        0, micro_count + n_section - 1, advance, (inflow_init, hidden_init, cache_init)
    )
    return (finished[1][None], finished[2][None])


def solution(mesh):
    in_specs = (
        P(None, "blk", "head"),
        P("section", "blk", None, "head"),
        P("section", None),
        P("section", None, None),
        P("section", None, None),
        P(),
        P(),
        P(),
        P("section", None, None, "blk", "head"),
    )
    out_specs = (P("section", None, "blk", "head"), P("section", None, None, "blk", "head"))
    return jax.shard_map(shards, mesh=mesh, in_specs=in_specs, out_specs=out_specs, check_vma=False)
```

profile of v0, /device:TPU:7, one launch (start us, length us, event | category | flops | bytes accessed | tf_op | source)
XLA Modules:
  0.0 475.2 jit_solution(3571729859346659106)
XLA Ops:
  8.6 2.4 all_gather.33
  11.0 1.4 fusion.25
  13.2 104.5 %all-gather.3.cloned.1.call-done = bf16[1,1536,3,768]{3,1,2,0:T(8,128)(2,1)} async-done(((bf16[1,192,3,768]{3,1,2,0:T(8,128)(2,1)}), bf16[1,1536,3,768]{3,1,2,0:T(8,128)(2,1)}) %all-gather.3.cloned.1.call-update) | async-done | bytes 7077904 | tf_op jit(solution)/shard_map/all_gather | solution.py:26
  117.7 4.0 fusion.28
  123.0 344.6 %while.20 = (s32[]{:T(128)}, bf16[8,1536]{1,0:T(8,128)(2,1)S(1)}, bf16[4,8,768]{2,1,0:T(8,128)(2,1)S(1)}, bf16[2,4,8,768]{3,2,1,0:T(8,128)(2,1)S(1)}, pred[]{:T(...) while((s32[]{:T(128)}, bf16[8,1536]{1,0:T(8,128)(2,1)S(1)}, ...), condition=%wide.region_8.9_spmd.clone, body=%wide.region_2.8_spmd.clone.sunk | while | flops 64782720 | bytes 9184839 | solution.py:111
  123.2 4.1 fusion.70
  129.7 21.1 %all_gather.41 = bf16[64,6,128]{2,0,1:T(8,128)(2,1)S(1)} all-gather(bf16[8,6,128]{2,0,1:T(8,128)(2,1)S(1)} %fusion.73), channel_id=1, replica_groups=mesh['section'=2,'blk'=8,'head'=2] {'blk'}, dimensions={0}, use_global_device_ids=true | all-gather | bytes 110592 | tf_op jit(solution)/shard_map/while/body/eval_jaxpr/all_gather | solution.py:90
  152.8 20.9 %all_gather.42 = bf16[64,6,128]{2,0,1:T(8,128)(2,1)S(1)} all-gather(bf16[8,6,128]{2,0,1:T(8,128)(2,1)S(1)} %slice_bitcast_fusion.5), channel_id=1, replica_groups=mesh['section'=2,'blk'=8,'head'=2] {'blk'}, dimensions={0}, use_global_device_ids=true | all-gather | bytes 110592 | tf_op jit(solution)/shard_map/while/body/eval_jaxpr/all_gather | solution.py:91
  174.7 11.5 %all_gather.43 = bf16[8,1536]{1,0:T(8,128)(2,1)S(1)} all-gather(bf16[8,768]{1,0:T(8,128)(2,1)S(1)} %get-tuple-element.663), channel_id=1, replica_groups=mesh['section'=2,'blk'=8,'head'=2] {'head'}, dimensions={1}, use_global_device_ids=true | all-gather | bytes 36864 | tf_op jit(solution)/shard_map/while/body/eval_jaxpr/all_gather | solution.py:107
  186.1 1.3 collective-permute-start
  187.5 3.2 collective-permute-done
  190.9 4.1 fusion.70
  197.3 21.2 %all_gather.41 = bf16[64,6,128]{2,0,1:T(8,128)(2,1)S(1)} all-gather(bf16[8,6,128]{2,0,1:T(8,128)(2,1)S(1)} %fusion.73), channel_id=1, replica_groups=mesh['section'=2,'blk'=8,'head'=2] {'blk'}, dimensions={0}, use_global_device_ids=true | all-gather | bytes 110592 | tf_op jit(solution)/shard_map/while/body/eval_jaxpr/all_gather | solution.py:90
  220.5 21.5 %all_gather.42 = bf16[64,6,128]{2,0,1:T(8,128)(2,1)S(1)} all-gather(bf16[8,6,128]{2,0,1:T(8,128)(2,1)S(1)} %slice_bitcast_fusion.5), channel_id=1, replica_groups=mesh['section'=2,'blk'=8,'head'=2] {'blk'}, dimensions={0}, use_global_device_ids=true | all-gather | bytes 110592 | tf_op jit(solution)/shard_map/while/body/eval_jaxpr/all_gather | solution.py:91
  242.9 12.5 %all_gather.43 = bf16[8,1536]{1,0:T(8,128)(2,1)S(1)} all-gather(bf16[8,768]{1,0:T(8,128)(2,1)S(1)} %get-tuple-element.663), channel_id=1, replica_groups=mesh['section'=2,'blk'=8,'head'=2] {'head'}, dimensions={1}, use_global_device_ids=true | all-gather | bytes 36864 | tf_op jit(solution)/shard_map/while/body/eval_jaxpr/all_gather | solution.py:107
  255.4 1.3 collective-permute-start
  256.7 3.2 collective-permute-done
  260.1 4.1 fusion.70
  266.5 21.2 %all_gather.41 = bf16[64,6,128]{2,0,1:T(8,128)(2,1)S(1)} all-gather(bf16[8,6,128]{2,0,1:T(8,128)(2,1)S(1)} %fusion.73), channel_id=1, replica_groups=mesh['section'=2,'blk'=8,'head'=2] {'blk'}, dimensions={0}, use_global_device_ids=true | all-gather | bytes 110592 | tf_op jit(solution)/shard_map/while/body/eval_jaxpr/all_gather | solution.py:90
  289.7 21.5 %all_gather.42 = bf16[64,6,128]{2,0,1:T(8,128)(2,1)S(1)} all-gather(bf16[8,6,128]{2,0,1:T(8,128)(2,1)S(1)} %slice_bitcast_fusion.5), channel_id=1, replica_groups=mesh['section'=2,'blk'=8,'head'=2] {'blk'}, dimensions={0}, use_global_device_ids=true | all-gather | bytes 110592 | tf_op jit(solution)/shard_map/while/body/eval_jaxpr/all_gather | solution.py:91
  312.1 12.5 %all_gather.43 = bf16[8,1536]{1,0:T(8,128)(2,1)S(1)} all-gather(bf16[8,768]{1,0:T(8,128)(2,1)S(1)} %get-tuple-element.663), channel_id=1, replica_groups=mesh['section'=2,'blk'=8,'head'=2] {'head'}, dimensions={1}, use_global_device_ids=true | all-gather | bytes 36864 | tf_op jit(solution)/shard_map/while/body/eval_jaxpr/all_gather | solution.py:107
  325.9 3.2 collective-permute-done
  329.3 4.1 fusion.70
  335.8 21.2 %all_gather.41 = bf16[64,6,128]{2,0,1:T(8,128)(2,1)S(1)} all-gather(bf16[8,6,128]{2,0,1:T(8,128)(2,1)S(1)} %fusion.73), channel_id=1, replica_groups=mesh['section'=2,'blk'=8,'head'=2] {'blk'}, dimensions={0}, use_global_device_ids=true | all-gather | bytes 110592 | tf_op jit(solution)/shard_map/while/body/eval_jaxpr/all_gather | solution.py:90
  359.0 21.5 %all_gather.42 = bf16[64,6,128]{2,0,1:T(8,128)(2,1)S(1)} all-gather(bf16[8,6,128]{2,0,1:T(8,128)(2,1)S(1)} %slice_bitcast_fusion.5), channel_id=1, replica_groups=mesh['section'=2,'blk'=8,'head'=2] {'blk'}, dimensions={0}, use_global_device_ids=true | all-gather | bytes 110592 | tf_op jit(solution)/shard_map/while/body/eval_jaxpr/all_gather | solution.py:91
  381.4 12.5 %all_gather.43 = bf16[8,1536]{1,0:T(8,128)(2,1)S(1)} all-gather(bf16[8,768]{1,0:T(8,128)(2,1)S(1)} %get-tuple-element.663), channel_id=1, replica_groups=mesh['section'=2,'blk'=8,'head'=2] {'head'}, dimensions={1}, use_global_device_ids=true | all-gather | bytes 36864 | tf_op jit(solution)/shard_map/while/body/eval_jaxpr/all_gather | solution.py:107
  395.2 3.2 collective-permute-done
  398.6 4.1 fusion.70
  405.0 21.2 %all_gather.41 = bf16[64,6,128]{2,0,1:T(8,128)(2,1)S(1)} all-gather(bf16[8,6,128]{2,0,1:T(8,128)(2,1)S(1)} %fusion.73), channel_id=1, replica_groups=mesh['section'=2,'blk'=8,'head'=2] {'blk'}, dimensions={0}, use_global_device_ids=true | all-gather | bytes 110592 | tf_op jit(solution)/shard_map/while/body/eval_jaxpr/all_gather | solution.py:90
  428.2 21.5 %all_gather.42 = bf16[64,6,128]{2,0,1:T(8,128)(2,1)S(1)} all-gather(bf16[8,6,128]{2,0,1:T(8,128)(2,1)S(1)} %slice_bitcast_fusion.5), channel_id=1, replica_groups=mesh['section'=2,'blk'=8,'head'=2] {'blk'}, dimensions={0}, use_global_device_ids=true | all-gather | bytes 110592 | tf_op jit(solution)/shard_map/while/body/eval_jaxpr/all_gather | solution.py:91
  450.6 12.5 %all_gather.43 = bf16[8,1536]{1,0:T(8,128)(2,1)S(1)} all-gather(bf16[8,768]{1,0:T(8,128)(2,1)S(1)} %get-tuple-element.663), channel_id=1, replica_groups=mesh['section'=2,'blk'=8,'head'=2] {'head'}, dimensions={1}, use_global_device_ids=true | all-gather | bytes 36864 | tf_op jit(solution)/shard_map/while/body/eval_jaxpr/all_gather | solution.py:107
  464.4 3.2 collective-permute-done
  (134 shorter events, 32.1 us)
Async XLA Ops:
  7.2 110.5 %all-gather.3.cloned.1.call-start = ((), (), s32[]{:S(2)}) async-start(), calls=%async_computation | async-start | bytes 7962624 | tf_op jit(solution)/shard_map/all_gather | solution.py:26
  121.7 1.3 copy-start.1
  121.7 1.3 copy-start.3
  121.7 1.3 copy-start.4
  186.1 4.6 collective-permute-start
  255.4 4.6 collective-permute-start
  324.6 4.6 collective-permute-start
  393.9 4.6 collective-permute-start
  463.1 4.6 collective-permute-start
  467.7 0.6 copy-start
  467.7 0.7 copy-start.2
Sparse Core Ops, SparseCore 0:
  10.2 107.4 all-gather.2
where the time goes:
time: 481 us; the launch traced here: 475 us
  blocking collectives  276 us (57%)
  waiting for transfers between devices  121 us (25%)
  matrix products  29.1 us (6%)
  other arithmetic  15 us (3%)
  between operations  14.2 us (3%)
  local copies, waits for them, and re-layouts  9.11 us (2%)
  starting transfers between devices  6.44 us (1%)
    all_gather x5, blocking collectives, advance(): piece_values = lax.all_gather(value_rows, 'blk', axis=0, tiled=True)  107 us
    all_gather x5, blocking collectives, advance(): piece_keys = lax.all_gather(key_rows, 'blk', axis=0, tiled=True)  106 us
    all_gather x1, waiting for transfers between devices, shards(): weights = lax.all_gather(w_qkv[0], 'blk', axis=0, tiled=True)  104 us
    all_gather x5, blocking collectives, advance(): whole_next = lax.all_gather(new_half, 'head', axis=1, tiled=True)  61.3 us
    dot_general x5, matrix products, advance(): jnp.einsum('td,dch->tch', normed, weights, preferred_element_type=jnp.flo...  20.3 us
    ppermute x5, waiting for transfers between devices, from_behind(): lax.ppermute(value, axis, [(source, source + steps) for source in range(f...  16.1 us
  transfers between devices with their start and end apart: 6, of which 6 were waited for; matrix products, arithmetic and copies ran while one was open for 1% of the time, Pallas kernels for 0%

commit v1 on v0

v1 whole, which is shorter than its diff:
```python
import functools

import jax
import jax.numpy as jnp
from jax import lax
from jax.experimental import pallas as pl
from jax.experimental.pallas import tpu as pltpu
from jax.sharding import PartitionSpec as P

MESH = pl.DeviceIdType.MESH
F32 = jnp.float32
BF16 = jnp.bfloat16


def rms(values, gain):
    return values * lax.rsqrt(jnp.mean(values * values, axis=-1, keepdims=True) + 1e-06) * gain


def kernel(
    dims,
    text_len, patch_len, flags,
    hid_in, w_in, row_gain, head_gain, text_in, stale_in,
    hid_out, cache_out,
    X, XN, TN, W, ST, TK, TV, hid_own, cache_own,
    zs, zr, ys, yr, ws, wr, ss, sr, hs, hr, cs, cr, one,
):
    S, B, heads, hd, micro, tok = dims
    off = (B - heads) // 2
    rows = micro * tok
    total = B * rows
    width = heads * hd
    depth = w_in.shape[1]
    s, b, h = lax.axis_index("section"), lax.axis_index("blk"), lax.axis_index("head")
    mate = b + 1 - 2 * lax.rem(b, 2)
    j_own = b - off
    owner = (b >= off) & (b < off + heads)
    half = pl.ds(pl.multiple_of(h * width, hd), width)
    other_half = pl.ds(pl.multiple_of((1 - h) * width, hd), width)

    def ahead(k):
        return lax.rem(b + k, B)

    def remote(src, dst, send, recv, dev):
        return pltpu.make_async_remote_copy(
            src_ref=src, dst_ref=dst, send_sem=send, recv_sem=recv, device_id=dev, device_id_type=MESH
        )

    def arrived(dst, sem):
        pltpu.make_async_copy(dst, dst, sem).wait()

    def push(src, dst, send, recv, target):
        @pl.when(target == b)
        def _():
            pltpu.make_async_copy(src, dst, recv).start()

        @pl.when(target != b)
        def _():
            remote(src, dst, send, recv, (s, target, h)).start()

    def pushed(src, send, target):
        @pl.when(target != b)
        def _():
            remote(src, src, send, send, (s, target, h)).wait_send()

    barrier = pltpu.get_barrier_semaphore()
    for k in range(1, B):
        pl.semaphore_signal(barrier, inc=1, device_id=(s, ahead(k), h), device_id_type=MESH)
    pl.semaphore_signal(barrier, inc=1, device_id=(s, b, 1 - h), device_id_type=MESH)

    @pl.when(s > 0)
    def _():
        pl.semaphore_signal(barrier, inc=1, device_id=(s - 1, b, h), device_id_type=MESH)

    @pl.when(s < S - 1)
    def _():
        pl.semaphore_signal(barrier, inc=1, device_id=(s + 1, b, h), device_id_type=MESH)

    pl.semaphore_wait(barrier, B + (s > 0).astype(jnp.int32) + (s < S - 1).astype(jnp.int32))

    def row_block(c):
        return X.at[c, :, half]

    def col_block(j):
        return X.at[:, :, pl.ds(pl.multiple_of(h * width + j * hd, hd), hd)]

    swap_cores = lambda: remote(X.at[:, :, half], X.at[:, :, half], one.at[0], one.at[1], (s, b, 1 - h))
    swap_in = lambda: arrived(X.at[:, :, other_half], one.at[1])

    @pl.when(s == 0)
    def _():
        pltpu.make_async_copy(hid_in, row_block(b), one.at[2]).start()
        for k in range(2, B, 2):
            remote(hid_in, row_block(b), zs.at[k], zr.at[b], (s, ahead(k), h)).start()
        remote(hid_in, row_block(b), ys.at[0], yr.at[b], (s, mate, h)).start()

    w_dst = W.at[pl.ds(pl.multiple_of(b * depth, depth), depth), :]
    st_dst = ST.at[:, b]
    for k in range(heads):
        j = lax.rem(b + k, heads)
        push(w_in.at[j], w_dst, ws.at[k], wr.at[b], j + off)
        st_src = stale_in.at[:, :, pl.ds(pl.multiple_of(j * hd, hd), hd)]
        push(st_src, st_dst, ss.at[k], sr.at[b], j + off)

    def norm_states():
        values = X[...].reshape(total, 2 * width).astype(F32)
        XN[...] = rms(values, row_gain[...]).astype(BF16)

    @pl.when(s == 0)
    def _():
        for k in range(2, B, 2):
            c = ahead(k)
            arrived(row_block(c), zr.at[c])
            remote(row_block(c), row_block(c), ys.at[k], yr.at[c], (s, mate, h)).start()
        pltpu.make_async_copy(hid_in, row_block(b), one.at[2]).wait()
        for k in range(0, B, 2):
            c = lax.rem(mate + k, B)
            arrived(row_block(c), yr.at[c])
        swap_cores().start()
        swap_in()

        @pl.when(owner)
        def _():
            norm_states()

    @pl.when(owner)
    def _():
        TN[...] = rms(text_in[...].astype(F32), row_gain[...]).astype(BF16)
        for c in range(B):
            arrived(W.at[pl.ds(c * depth, depth), :], wr.at[c])
        text_kv = jnp.dot(TN[...], W[:, hd:], preferred_element_type=F32).astype(BF16)
        TK[...] = rms(text_kv[:, :hd].astype(F32), head_gain[1:2, :]).astype(BF16)
        TV[...] = text_kv[:, hd:]
        for c in range(B):
            arrived(ST.at[:, c], sr.at[c])

    @pl.when(s > 0)
    def _():
        @pl.when(owner)
        def _():
            mine = col_block(j_own)
            arrived(mine, one.at[3])
            for k in range(2, B, 2):
                remote(mine, mine, zs.at[k], zr.at[b], (s, ahead(k), h)).start()
            remote(mine, mine, ys.at[0], yr.at[b], (s, mate, h)).start()

        for k in range(2, B, 2):
            c = ahead(k)

            @pl.when((c >= off) & (c < off + heads))
            def _():
                block = col_block(c - off)
                arrived(block, zr.at[c])
                remote(block, block, ys.at[k], yr.at[c], (s, mate, h)).start()

        for k in range(0, B, 2):
            c = lax.rem(mate + k, B)

            @pl.when((c >= off) & (c < off + heads))
            def _():
                arrived(col_block(c - off), yr.at[c])

        swap_cores().start()
        swap_in()

        @pl.when(owner)
        def _():
            norm_states()

    @pl.when(owner)
    def _():
        proj = jnp.dot(XN[...], W[...], preferred_element_type=F32)
        fresh_k = proj[:, hd : 2 * hd].astype(BF16)
        fresh_v = proj[:, 2 * hd :].astype(BF16)
        cache_own[0] = fresh_k.reshape(B, rows, hd)
        cache_own[1] = fresh_v.reshape(B, rows, hd)
        tok_bits = tok.bit_length() - 1

        def place(shape, axis):
            at = lax.broadcasted_iota(jnp.int32, shape, axis)
            which = lax.shift_right_logical(at, tok_bits) & (micro - 1)
            spot = lax.shift_right_logical(at, rows.bit_length() - 1) * tok + (at & (tok - 1))
            return which, spot

        def per_micro(which, read):
            out = jnp.zeros(which.shape, jnp.int32)
            for m in range(micro):
                out = jnp.where(which == m, read(m), out)
            return out

        which, _ = place((total, hd), 0)
        use_stale = per_micro(which, lambda m: flags[m, s]) == 1
        kept_k = jnp.where(use_stale, ST[0].reshape(total, hd).astype(F32), fresh_k.astype(F32))
        kept_v = jnp.where(use_stale, ST[1].reshape(total, hd).astype(F32), fresh_v.astype(F32))
        keys = rms(kept_k, head_gain[1:2, :]).astype(BF16)
        queries = rms(proj[:, :hd], head_gain[0:1, :]).astype(BF16)
        scale = hd**-0.5
        nt = (((1,), (1,)), ((), ()))

        def attend(key_rows, value_rows, mask):
            scores = lax.dot_general(queries, key_rows, nt, preferred_element_type=F32) * scale
            probs = jnp.where(mask, jnp.exp(scores), 0.0)
            num = jnp.dot(probs.astype(BF16), value_rows, preferred_element_type=F32)
            return num, jnp.sum(probs, axis=1, keepdims=True)

        shape = (total, total)
        q_which, _ = place(shape, 0)
        k_which, k_spot = place(shape, 1)
        mask = (q_which == k_which) & (k_spot < per_micro(k_which, lambda m: patch_len[m]))
        num, den = attend(keys, kept_v.astype(BF16), mask)
        text_at = lax.broadcasted_iota(jnp.int32, (total, TK.shape[0]), 1)
        text_num, text_den = attend(TK[...], TV[...], text_at < text_len[0])
        attended = (num + text_num) / (den + text_den)
        state = X[:, :, pl.ds(pl.multiple_of(h * width + j_own * hd, hd), hd)]
        new = (state.reshape(total, hd).astype(F32) + attended).astype(BF16)
        hid_own[...] = new.reshape(B, rows, hd)

        @pl.when(s < S - 1)
        def _():
            remote(hid_own, col_block(j_own), one.at[4], one.at[3], (s + 1, b, h)).start()

        cols = pl.ds(pl.multiple_of(j_own * hd, hd), hd)
        for k in range(B):
            t = ahead(k)
            push(hid_own.at[t], hid_out.at[:, cols], hs.at[k], hr.at[j_own], t)
            push(cache_own.at[:, t], cache_out.at[:, :, cols], cs.at[k], cr.at[j_own], t)
        for k in range(B):
            t = ahead(k)
            pushed(hid_own.at[t], hs.at[k], t)
            pushed(cache_own.at[:, t], cs.at[k], t)

        @pl.when(s < S - 1)
        def _():
            remote(hid_own, col_block(j_own), one.at[4], one.at[3], (s + 1, b, h)).wait_send()

    for j in range(heads):
        cols = pl.ds(j * hd, hd)
        arrived(hid_out.at[:, cols], hr.at[j])
        arrived(cache_out.at[:, :, cols], cr.at[j])

    for k in range(heads):
        j = lax.rem(b + k, heads)
        pushed(w_in.at[j], ws.at[k], j + off)
        pushed(stale_in.at[:, :, pl.ds(pl.multiple_of(j * hd, hd), hd)], ss.at[k], j + off)
    swap_cores().wait_send()

    @pl.when(s == 0)
    def _():
        for k in range(2, B, 2):
            remote(hid_in, row_block(b), zs.at[k], zr.at[b], (s, ahead(k), h)).wait_send()
        for k in range(0, B, 2):
            remote(hid_in, row_block(b), ys.at[k], yr.at[b], (s, mate, h)).wait_send()

    @pl.when(s > 0)
    def _():
        block = col_block(0)

        @pl.when(owner)
        def _():
            for k in range(2, B, 2):
                remote(block, block, zs.at[k], zr.at[b], (s, ahead(k), h)).wait_send()

        for k in range(0, B, 2):
            c = ahead(k)

            @pl.when((c >= off) & (c < off + heads))
            def _():
                remote(block, block, ys.at[k], yr.at[b], (s, mate, h)).wait_send()


def shards(
    hidden_in, w_qkv, norm_gain, qk_gain, text_states, text_len, patch_len, stale_flags, stale_kv
):
    S, B = lax.axis_size("section"), lax.axis_size("blk")
    micro, tok, width = hidden_in.shape
    hd = qk_gain.shape[2]
    heads = width // hd
    rows = micro * tok
    total = B * rows
    depth = w_qkv.shape[1]
    text = text_states.shape[1]
    w = w_qkv[0].reshape(depth, 3, heads, hd).transpose(2, 0, 1, 3).reshape(heads, depth, 3 * hd)
    smem = pl.BlockSpec(memory_space=pltpu.SMEM)
    vmem = pl.BlockSpec(memory_space=pltpu.VMEM)
    sem = pltpu.SemaphoreType.DMA
    hid, cache = pl.pallas_call(
        functools.partial(kernel, (S, B, heads, hd, micro, tok)),
        out_shape=(
            jax.ShapeDtypeStruct((rows, width), BF16),
            jax.ShapeDtypeStruct((2, rows, width), BF16),
        ),
        in_specs=[smem] * 3 + [vmem] * 6,
        out_specs=(vmem, vmem),
        scratch_shapes=[
            pltpu.VMEM((B, rows, 2 * width), BF16),
            pltpu.VMEM((total, 2 * width), BF16),
            pltpu.VMEM((text, 2 * width), BF16),
            pltpu.VMEM((B * depth, 3 * hd), BF16),
            pltpu.VMEM((2, B, rows, hd), BF16),
            pltpu.VMEM((text, hd), BF16),
            pltpu.VMEM((text, hd), BF16),
            pltpu.VMEM((B, rows, hd), BF16),
            pltpu.VMEM((2, B, rows, hd), BF16),
            sem((B,)), sem((B,)), sem((B,)), sem((B,)),
            sem((heads,)), sem((B,)), sem((heads,)), sem((B,)),
            sem((B,)), sem((heads,)), sem((B,)), sem((heads,)),
            sem((5,)),
        ],
        compiler_params=pltpu.CompilerParams(
            collective_id=0, has_side_effects=True, vmem_limit_bytes=60 * 1024 * 1024
        ),
    )(
        text_len, patch_len, stale_flags,
        hidden_in.reshape(rows, width), w, norm_gain, qk_gain[0], text_states[0],
        stale_kv[0].reshape(2, rows, width),
    )
    return (
        hid.reshape(1, micro, tok, width),
        cache.reshape(1, 2, micro, tok, width),
    )


def solution(mesh):
    in_specs = (
        P(None, "blk", "head"),
        P("section", "blk", None, "head"),
        P("section", None),
        P("section", None, None),
        P("section", None, None),
        P(),
        P(),
        P(),
        P("section", None, None, "blk", "head"),
    )
    out_specs = (P("section", None, "blk", "head"), P("section", None, None, "blk", "head"))
    return jax.shard_map(shards, mesh=mesh, in_specs=in_specs, out_specs=out_specs, check_vma=False)
```

time: 481 us -> 64.5 us (0.13); the launches traced: 475 us -> 64.2 us
  blocking collectives: 276 us -> 0 us
  waiting for transfers between devices: 121 us -> 0 us
  Pallas kernels: 0 us -> 54.5 us
  matrix products: 29.1 us -> 0 us
  other arithmetic: 15 us -> 0 us
  between operations: 14.2 us -> 1.31 us
  starting transfers between devices: 6.44 us -> 0 us
    all_gather x16 -> x0, blocking collectives: 276 us -> none  [the longest x5 107 us: advance(): piece_values = lax.all_gather(value_rows, 'blk', axis=0, tiled=True)]
    all_gather x1 -> x0, waiting for transfers between devices: 104 us -> none  [shards(): weights = lax.all_gather(w_qkv[0], 'blk', axis=0, tiled=True)]
    pallas_call x0 -> x1, Pallas kernels: none -> 54.5 us  [shards(): pl.pallas_call(functools.partial(kernel, (S, B, heads, hd, micro, tok)),...]
    dot_general x26 -> x0, matrix products: 29.1 us -> none  [the longest x5 20.3 us: advance(): jnp.einsum('td,dch->tch', normed, weights, preferred_element_type=jnp.flo...]
    ppermute x5 -> x0, waiting for transfers between devices: 16.1 us -> none  [from_behind(): lax.ppermute(value, axis, [(source, source + steps) for source in range(f...]
    lt x10 -> x0, other arithmetic: 6.72 us -> none  [the longest x5 3.46 us: advance(): key_mask = jnp.arange(piece_keys.shape[0]) < patch_limit]
    dynamic_slice x10 -> x0, local copies, waits for them, and re-layouts: 6.71 us -> none  [the longest x5 3.36 us: advance(): lax.dynamic_slice(stale_flags, (micro_at, section_idx), (1, 1))[0, 0]]
    ppermute x5 -> x0, starting transfers between devices: 6.4 us -> none  [from_behind(): lax.ppermute(value, axis, [(source, source + steps) for source in range(f...]
  transfers between devices with their start and end apart: 6 -> 0, of which waited for: 6 -> 0; matrix products, arithmetic and copies ran while one was open for 1% -> 0% of each run, Pallas kernels for 0% -> 0%
where the time goes in v1:
time: 64.5 us; the launch traced here: 64.2 us
  Pallas kernels  54.5 us (84%)
  local copies, waits for them, and re-layouts  8.4 us (13%)
  between operations  1.31 us (2%)
    pallas_call x1, Pallas kernels, shards(): pl.pallas_call(functools.partial(kernel, (S, B, heads, hd, micro, tok)),...  54.5 us
    unnamed x5, local copies, waits for them, and re-layouts  3.63 us
    another operation x1, local copies, waits for them, and re-layouts, shards(): w_qkv[0].reshape(depth, 3, heads, hd).transpose(2, 0, 1, 3)  2.08 us
    reshape x1, local copies, waits for them, and re-layouts, shards(): w_qkv[0].reshape(depth, 3, heads, hd).transpose(2, 0, 1, 3)  1.93 us

profile of v1, /device:TPU:7, one launch (start us, length us, event | category | flops | bytes accessed | tf_op | source)
XLA Modules:
  0.0 64.2 jit_solution(11480362981416890961)
XLA Ops:
  0.6 2.1 %reshape_squeeze.6 = bf16[192,3,6,128]{3,2,0,1:T(8,128)(2,1)S(1)} reshape(bf16[1,192,3,768]{3,1,2,0:T(8,128)(2,1)} %param.10) | data formatting | bytes 1769472 | tf_op jit(solution)/shard_map/reshape;squeeze | solution.py:281
  2.7 0.8 %copy.13 = bf16[6,192,3,128]{3,2,1,0:T(4,128)(2,1)S(1)} copy(bf16[6,192,3,128]{3,0,1,2:T(8,128)(2,1)S(1)} %bitcast.11) | data formatting | bytes 1769472 | tf_op jit(solution)/shard_map/transpose | solution.py:281
  3.5 0.0 copy-start
  3.5 1.9 %reshape.17.w_in = bf16[6,192,384]{2,1,0:T(8,128)(2,1)} reshape(bf16[6,192,3,128]{3,2,1,0:T(4,128)(2,1)S(1)} %copy.13) | data formatting | bytes 1769472 | tf_op jit(solution)/shard_map/reshape | solution.py:281
  5.4 0.0 copy-done
  5.4 0.7 %copy.14.flags = s32[4,2]{1,0:T(4,128)} copy(s32[4,2]{0,1:T(2,128)S(1)} %copy-done) | data formatting | bytes 64 | tf_op args[7]
  6.7 54.5 %shard_map.104 = (bf16[32,768]{1,0:T(8,128)(2,1)}, bf16[2,32,768]{2,1,0:T(8,128)(2,1)}) custom-call(s32[1]{0:T(128)S(6)} %copy.17.text_len, s32[4]{0:T(128)} %patch_len.1, s32[4,2]{1,0:T(4,128)} %copy.14.flags, bf16[32,768]{1,0:T(8,128)(2,1)} %bitcast.16, bf16[6,192,384]{2,1,0:T(8,128)(2,1)} %reshape.17.w_in, f32[1,1536]{1,0:T(1,128)} %row_gain.1, ...), custom_call_target="tpu_custom_call" | custom-call | tf_op jit(solution)/shard_map/pallas_call | solution.py:285
  61.3 1.4 %copy.18 = bf16[1,4,8,768]{3,2,1,0:T(8,128)(2,1)} copy(bf16[1,4,8,768]{3,2,1,0:T(8,128)(2,1)} %bitcast.15) | data formatting | bytes 98304
  62.7 1.5 %copy.19 = bf16[1,2,4,8,768]{4,3,2,1,0:T(8,128)(2,1)} copy(bf16[1,2,4,8,768]{4,3,2,1,0:T(8,128)(2,1)} %bitcast.14) | data formatting | bytes 196608
Async XLA Ops:
  3.5 1.9 %copy-start = (s32[4,2]{0,1:T(2,128)S(1)}, s32[4,2]{0,1:T(2,128)}, u32[]{:S(2)}) copy-start(s32[4,2]{0,1:T(2,128)} %param.16) | copy-start | bytes 100

commit v2 on v1

--- a/solution.py
+++ b/solution.py
@@ -21,8 +21,8 @@
     text_len, patch_len, flags,
     hid_in, w_in, row_gain, head_gain, text_in, stale_in,
     hid_out, cache_out,
-    X, XN, TN, W, ST, TK, TV, hid_own, cache_own,
-    zs, zr, ys, yr, ws, wr, ss, sr, hs, hr, cs, cr, one,
+    X, G, XN, TN, W, ST, TK, TV, hid_own, cache_own,
+    zs, zr, ys, yr, ws, wr, ss, sr, hs, hr, cs, cr, gzs, gzr, gys, gyr, gxs, one,
 ):
     S, B, heads, hd, micro, tok = dims
     off = (B - heads) // 2
@@ -89,17 +89,37 @@
     @pl.when(s == 0)
     def _():
         pltpu.make_async_copy(hid_in, row_block(b), one.at[2]).start()
+
+    @pl.when(s == 1)
+    def _():
+        def hand_over(c, k):
+            remote(G.at[c], row_block(c), gxs.at[k], yr.at[c], (s - 1, b, h)).start()
+
         for k in range(2, B, 2):
-            remote(hid_in, row_block(b), zs.at[k], zr.at[b], (s, ahead(k), h)).start()
-        remote(hid_in, row_block(b), ys.at[0], yr.at[b], (s, mate, h)).start()
-
-    w_dst = W.at[pl.ds(pl.multiple_of(b * depth, depth), depth), :]
+            remote(hid_in, G.at[b], gzs.at[k], gzr.at[b], (s, ahead(k), h)).start()
+        remote(hid_in, G.at[b], gys.at[0], gyr.at[b], (s, mate, h)).start()
+        for k in range(2, B, 2):
+            c = ahead(k)
+            arrived(G.at[c], gzr.at[c])
+            remote(G.at[c], G.at[c], gys.at[k], gyr.at[c], (s, mate, h)).start()
+            hand_over(c, k)
+        for k in range(0, B, 2):
+            c = lax.rem(mate + k, B)
+            arrived(G.at[c], gyr.at[c])
+            hand_over(c, k + 1)
+
+    w_dst = W.at[:, pl.ds(pl.multiple_of(b * depth, depth), depth), :]
     st_dst = ST.at[:, b]
+
+    def cols_of(j):
+        return pl.ds(pl.multiple_of(j * hd, hd), hd)
+
     for k in range(heads):
         j = lax.rem(b + k, heads)
-        push(w_in.at[j], w_dst, ws.at[k], wr.at[b], j + off)
-        st_src = stale_in.at[:, :, pl.ds(pl.multiple_of(j * hd, hd), hd)]
-        push(st_src, st_dst, ss.at[k], sr.at[b], j + off)
+        push(w_in.at[:, :, cols_of(j)], w_dst, ws.at[k], wr.at[b], j + off)
+    for k in range(heads):
+        j = lax.rem(b + k, heads)
+        push(stale_in.at[:, :, cols_of(j)], st_dst, ss.at[k], sr.at[b], j + off)
 
     def norm_states():
         values = X[...].reshape(total, 2 * width).astype(F32)
@@ -107,14 +127,9 @@
 
     @pl.when(s == 0)
     def _():
-        for k in range(2, B, 2):
-            c = ahead(k)
-            arrived(row_block(c), zr.at[c])
-            remote(row_block(c), row_block(c), ys.at[k], yr.at[c], (s, mate, h)).start()
         pltpu.make_async_copy(hid_in, row_block(b), one.at[2]).wait()
-        for k in range(0, B, 2):
-            c = lax.rem(mate + k, B)
-            arrived(row_block(c), yr.at[c])
+        for k in range(1, B):
+            arrived(row_block(ahead(k)), yr.at[ahead(k)])
         swap_cores().start()
         swap_in()
 
@@ -126,12 +141,12 @@
     def _():
         TN[...] = rms(text_in[...].astype(F32), row_gain[...]).astype(BF16)
         for c in range(B):
-            arrived(W.at[pl.ds(c * depth, depth), :], wr.at[c])
-        text_kv = jnp.dot(TN[...], W[:, hd:], preferred_element_type=F32).astype(BF16)
+            arrived(W.at[:, pl.ds(c * depth, depth), :], wr.at[c])
+        text_kv = jnp.dot(
+            TN[...], jnp.concatenate([W[1], W[2]], axis=1), preferred_element_type=F32
+        ).astype(BF16)
         TK[...] = rms(text_kv[:, :hd].astype(F32), head_gain[1:2, :]).astype(BF16)
         TV[...] = text_kv[:, hd:]
-        for c in range(B):
-            arrived(ST.at[:, c], sr.at[c])
 
     @pl.when(s > 0)
     def _():
@@ -168,11 +183,19 @@
 
     @pl.when(owner)
     def _():
-        proj = jnp.dot(XN[...], W[...], preferred_element_type=F32)
+        proj = jnp.dot(
+            XN[...], jnp.concatenate([W[0], W[1], W[2]], axis=1), preferred_element_type=F32
+        )
         fresh_k = proj[:, hd : 2 * hd].astype(BF16)
         fresh_v = proj[:, 2 * hd :].astype(BF16)
         cache_own[0] = fresh_k.reshape(B, rows, hd)
         cache_own[1] = fresh_v.reshape(B, rows, hd)
+        cols = cols_of(j_own)
+        for k in range(B):
+            t = ahead(k)
+            push(cache_own.at[:, t], cache_out.at[:, :, cols], cs.at[k], cr.at[j_own], t)
+        for c in range(B):
+            arrived(ST.at[:, c], sr.at[c])
         tok_bits = tok.bit_length() - 1
 
         def place(shape, axis):
@@ -188,7 +211,7 @@
             return out
 
         which, _ = place((total, hd), 0)
-        use_stale = per_micro(which, lambda m: flags[m, s]) == 1
+        use_stale = per_micro(which, lambda m: flags[s, m]) == 1
         kept_k = jnp.where(use_stale, ST[0].reshape(total, hd).astype(F32), fresh_k.astype(F32))
         kept_v = jnp.where(use_stale, ST[1].reshape(total, hd).astype(F32), fresh_v.astype(F32))
         keys = rms(kept_k, head_gain[1:2, :]).astype(BF16)
@@ -218,11 +241,9 @@
         def _():
             remote(hid_own, col_block(j_own), one.at[4], one.at[3], (s + 1, b, h)).start()
 
-        cols = pl.ds(pl.multiple_of(j_own * hd, hd), hd)
         for k in range(B):
             t = ahead(k)
             push(hid_own.at[t], hid_out.at[:, cols], hs.at[k], hr.at[j_own], t)
-            push(cache_own.at[:, t], cache_out.at[:, :, cols], cs.at[k], cr.at[j_own], t)
         for k in range(B):
             t = ahead(k)
             pushed(hid_own.at[t], hs.at[k], t)
@@ -239,16 +260,18 @@
 
     for k in range(heads):
         j = lax.rem(b + k, heads)
-        pushed(w_in.at[j], ws.at[k], j + off)
-        pushed(stale_in.at[:, :, pl.ds(pl.multiple_of(j * hd, hd), hd)], ss.at[k], j + off)
+        pushed(w_in.at[:, :, cols_of(j)], ws.at[k], j + off)
+        pushed(stale_in.at[:, :, cols_of(j)], ss.at[k], j + off)
     swap_cores().wait_send()
 
-    @pl.when(s == 0)
-    def _():
+    @pl.when(s == 1)
+    def _():
+        for k in range(1, B):
+            remote(G.at[b], G.at[b], gxs.at[k], gyr.at[b], (s - 1, b, h)).wait_send()
         for k in range(2, B, 2):
-            remote(hid_in, row_block(b), zs.at[k], zr.at[b], (s, ahead(k), h)).wait_send()
+            remote(G.at[b], G.at[b], gzs.at[k], gzr.at[b], (s, ahead(k), h)).wait_send()
         for k in range(0, B, 2):
-            remote(hid_in, row_block(b), ys.at[k], yr.at[b], (s, mate, h)).wait_send()
+            remote(G.at[b], G.at[b], gys.at[k], gyr.at[b], (s, mate, h)).wait_send()
 
     @pl.when(s > 0)
     def _():
@@ -278,7 +301,7 @@
     total = B * rows
     depth = w_qkv.shape[1]
     text = text_states.shape[1]
-    w = w_qkv[0].reshape(depth, 3, heads, hd).transpose(2, 0, 1, 3).reshape(heads, depth, 3 * hd)
+    w = w_qkv[0].transpose(1, 0, 2)
     smem = pl.BlockSpec(memory_space=pltpu.SMEM)
     vmem = pl.BlockSpec(memory_space=pltpu.VMEM)
     sem = pltpu.SemaphoreType.DMA
@@ -292,9 +315,10 @@
         out_specs=(vmem, vmem),
         scratch_shapes=[
             pltpu.VMEM((B, rows, 2 * width), BF16),
+            pltpu.VMEM((B, rows, width), BF16),
             pltpu.VMEM((total, 2 * width), BF16),
             pltpu.VMEM((text, 2 * width), BF16),
-            pltpu.VMEM((B * depth, 3 * hd), BF16),
+            pltpu.VMEM((3, B * depth, hd), BF16),
             pltpu.VMEM((2, B, rows, hd), BF16),
             pltpu.VMEM((text, hd), BF16),
             pltpu.VMEM((text, hd), BF16),
@@ -303,13 +327,14 @@
             sem((B,)), sem((B,)), sem((B,)), sem((B,)),
             sem((heads,)), sem((B,)), sem((heads,)), sem((B,)),
             sem((B,)), sem((heads,)), sem((B,)), sem((heads,)),
+            sem((B,)), sem((B,)), sem((B,)), sem((B,)), sem((B + 1,)),
             sem((5,)),
         ],
         compiler_params=pltpu.CompilerParams(
             collective_id=0, has_side_effects=True, vmem_limit_bytes=60 * 1024 * 1024
         ),
     )(
-        text_len, patch_len, stale_flags,
+        text_len, patch_len, stale_flags.T,
         hidden_in.reshape(rows, width), w, norm_gain, qk_gain[0], text_states[0],
         stale_kv[0].reshape(2, rows, width),
     )

time: 64.5 us -> 63.1 us (0.978); the launches traced: 64.2 us -> 62.1 us
  local copies, waits for them, and re-layouts: 8.4 us -> 2.1 us
  Pallas kernels: 54.5 us -> 58.7 us
    pallas_call x1, Pallas kernels: 54.5 us -> 58.7 us  [shards(): pl.pallas_call(functools.partial(kernel, (S, B, heads, hd, micro, tok)),...]
    another operation x1 -> x0, local copies, waits for them, and re-layouts: 2.08 us -> none  [shards(): w_qkv[0].reshape(depth, 3, heads, hd).transpose(2, 0, 1, 3)]
    reshape x1 -> x0, local copies, waits for them, and re-layouts: 1.93 us -> none  [shards(): w_qkv[0].reshape(depth, 3, heads, hd).transpose(2, 0, 1, 3)]
    unnamed x5 -> x4, local copies, waits for them, and re-layouts: 3.63 us -> 2.1 us
    transpose x1 -> x0, local copies, waits for them, and re-layouts: 0.76 us -> none  [shards(): w_qkv[0].reshape(depth, 3, heads, hd).transpose(2, 0, 1, 3)]
where the time goes in v2:
time: 63.1 us; the launch traced here: 62.1 us
  Pallas kernels  58.7 us (93%)
  local copies, waits for them, and re-layouts  2.1 us (3%)
  between operations  1.29 us (2%)
    pallas_call x1, Pallas kernels, shards(): pl.pallas_call(functools.partial(kernel, (S, B, heads, hd, micro, tok)),...  58.7 us
    unnamed x4, local copies, waits for them, and re-layouts  2.1 us

profile of v2, /device:TPU:7, one launch (start us, length us, event | category | flops | bytes accessed | tf_op | source)
XLA Modules:
  0.0 62.1 jit_solution(14376137058673201572)
XLA Ops:
  1.3 58.7 %shard_map.104 = (bf16[32,768]{1,0:T(8,128)(2,1)}, bf16[2,32,768]{2,1,0:T(8,128)(2,1)}) custom-call(s32[1]{0:T(128)S(6)} %copy.13.text_len, s32[4]{0:T(128)} %patch_len.1, s32[2,4]{1,0:T(2,128)} %bitcast.16, bf16[32,768]{1,0:T(8,128)(2,1)} %bitcast.15, bf16[3,192,768]{2,1,0:T(8,128)(2,1)} %bitcast.10, f32[1,1536]{1,0:T(1,128)} %row_gain.1, ...), custom_call_target="tpu_custom_call" | custom-call | tf_op jit(solution)/shard_map/pallas_call | solution.py:308
  60.0 0.0 copy-start
  60.0 1.5 %copy.14 = bf16[1,4,8,768]{3,2,1,0:T(8,128)(2,1)} copy(bf16[1,4,8,768]{3,2,1,0:T(8,128)(2,1)} %bitcast.14) | data formatting | bytes 98304
  61.4 0.0 copy-done
  61.4 0.6 %copy.15 = bf16[1,2,4,8,768]{4,3,2,1,0:T(8,128)(2,1)} copy(bf16[1,2,4,8,768]{4,3,2,1,0:T(8,128)(2,1)S(1)} %bitcast.13) | data formatting | bytes 196608
Async XLA Ops:
  60.0 1.5 %copy-start = (bf16[2,32,768]{2,1,0:T(8,128)(2,1)S(1)}, bf16[2,32,768]{2,1,0:T(8,128)(2,1)}, u32[]{:S(2)}) copy-start(bf16[2,32,768]{2,1,0:T(8,128)(2,1)} %get-tuple-element.5) | copy-start | bytes 294916

commit v3 on v2

--- a/solution.py
+++ b/solution.py
@@ -19,9 +19,9 @@
 def kernel(
     dims,
     text_len, patch_len, flags,
-    hid_in, w_in, row_gain, head_gain, text_in, stale_in,
+    hid_in, w_in, row_gain, head_gain, text_hbm, stale_in,
     hid_out, cache_out,
-    X, G, XN, TN, W, ST, TK, TV, hid_own, cache_own,
+    X, X1, RES, G, XN, text_in, TN, W, ST, TK, TV, hid_own, cache_own,
     zs, zr, ys, yr, ws, wr, ss, sr, hs, hr, cs, cr, gzs, gzr, gys, gyr, gxs, one,
 ):
     S, B, heads, hd, micro, tok = dims
@@ -62,6 +62,8 @@
         def _():
             remote(src, src, send, send, (s, target, h)).wait_send()
 
+    text_copy = pltpu.make_async_copy(text_hbm, text_in, one.at[5])
+    text_copy.start()
     barrier = pltpu.get_barrier_semaphore()
     for k in range(1, B):
         pl.semaphore_signal(barrier, inc=1, device_id=(s, ahead(k), h), device_id_type=MESH)
@@ -81,10 +83,13 @@
         return X.at[c, :, half]
 
     def col_block(j):
-        return X.at[:, :, pl.ds(pl.multiple_of(h * width + j * hd, hd), hd)]
-
-    swap_cores = lambda: remote(X.at[:, :, half], X.at[:, :, half], one.at[0], one.at[1], (s, b, 1 - h))
-    swap_in = lambda: arrived(X.at[:, :, other_half], one.at[1])
+        return X1.at[h, j]
+
+    def swap_cores():
+        return remote(X.at[:, :, half], X.at[:, :, half], one.at[0], one.at[1], (s, b, 1 - h))
+
+    def swap_blocks():
+        return remote(X1.at[h], X1.at[h], one.at[0], one.at[1], (s, b, 1 - h))
 
     @pl.when(s == 0)
     def _():
@@ -92,21 +97,20 @@
 
     @pl.when(s == 1)
     def _():
-        def hand_over(c, k):
-            remote(G.at[c], row_block(c), gxs.at[k], yr.at[c], (s - 1, b, h)).start()
-
         for k in range(2, B, 2):
             remote(hid_in, G.at[b], gzs.at[k], gzr.at[b], (s, ahead(k), h)).start()
         remote(hid_in, G.at[b], gys.at[0], gyr.at[b], (s, mate, h)).start()
+
+    def hand_over(c, k):
+        remote(G.at[c], row_block(c), gxs.at[k], yr.at[c], (s - 1, b, h)).start()
+
+    @pl.when(s == 1)
+    def _():
         for k in range(2, B, 2):
             c = ahead(k)
             arrived(G.at[c], gzr.at[c])
             remote(G.at[c], G.at[c], gys.at[k], gyr.at[c], (s, mate, h)).start()
             hand_over(c, k)
-        for k in range(0, B, 2):
-            c = lax.rem(mate + k, B)
-            arrived(G.at[c], gyr.at[c])
-            hand_over(c, k + 1)
 
     w_dst = W.at[:, pl.ds(pl.multiple_of(b * depth, depth), depth), :]
     st_dst = ST.at[:, b]
@@ -121,8 +125,15 @@
         j = lax.rem(b + k, heads)
         push(stale_in.at[:, :, cols_of(j)], st_dst, ss.at[k], sr.at[b], j + off)
 
-    def norm_states():
-        values = X[...].reshape(total, 2 * width).astype(F32)
+    @pl.when(s == 1)
+    def _():
+        for k in range(0, B, 2):
+            c = lax.rem(mate + k, B)
+            arrived(G.at[c], gyr.at[c])
+            hand_over(c, k + 1)
+
+    def norm_states(values):
+        values = values.astype(F32)
         XN[...] = rms(values, row_gain[...]).astype(BF16)
 
     @pl.when(s == 0)
@@ -131,11 +142,14 @@
         for k in range(1, B):
             arrived(row_block(ahead(k)), yr.at[ahead(k)])
         swap_cores().start()
-        swap_in()
+        arrived(X.at[:, :, other_half], one.at[1])
 
         @pl.when(owner)
         def _():
-            norm_states()
+            norm_states(X[...].reshape(total, 2 * width))
+            RES[...] = X[:, :, pl.ds(pl.multiple_of(h * width + j_own * hd, hd), hd)].reshape(total, hd)
+
+    text_copy.wait()
 
     @pl.when(owner)
     def _():
@@ -174,12 +188,15 @@
             def _():
                 arrived(col_block(c - off), yr.at[c])
 
-        swap_cores().start()
-        swap_in()
+        swap_blocks().start()
+        arrived(X1.at[1 - h], one.at[1])
 
         @pl.when(owner)
         def _():
-            norm_states()
+            norm_states(
+                jnp.concatenate([X1[i, j] for i in range(2) for j in range(heads)], axis=1)
+            )
+            RES[...] = X1[h, j_own]
 
     @pl.when(owner)
     def _():
@@ -233,9 +250,7 @@
         text_at = lax.broadcasted_iota(jnp.int32, (total, TK.shape[0]), 1)
         text_num, text_den = attend(TK[...], TV[...], text_at < text_len[0])
         attended = (num + text_num) / (den + text_den)
-        state = X[:, :, pl.ds(pl.multiple_of(h * width + j_own * hd, hd), hd)]
-        new = (state.reshape(total, hd).astype(F32) + attended).astype(BF16)
-        hid_own[...] = new.reshape(B, rows, hd)
+        hid_own[...] = (RES[...].astype(F32) + attended).astype(BF16)
 
         @pl.when(s < S - 1)
         def _():
@@ -243,10 +258,10 @@
 
         for k in range(B):
             t = ahead(k)
-            push(hid_own.at[t], hid_out.at[:, cols], hs.at[k], hr.at[j_own], t)
+            push(hid_own.at[pl.ds(pl.multiple_of(t * rows, rows), rows), :], hid_out.at[:, cols], hs.at[k], hr.at[j_own], t)
         for k in range(B):
             t = ahead(k)
-            pushed(hid_own.at[t], hs.at[k], t)
+            pushed(hid_own.at[pl.ds(0, rows), :], hs.at[k], t)
             pushed(cache_own.at[:, t], cs.at[k], t)
 
         @pl.when(s < S - 1)
@@ -304,6 +319,7 @@
     w = w_qkv[0].transpose(1, 0, 2)
     smem = pl.BlockSpec(memory_space=pltpu.SMEM)
     vmem = pl.BlockSpec(memory_space=pltpu.VMEM)
+    hbm = pl.BlockSpec(memory_space=pl.ANY)
     sem = pltpu.SemaphoreType.DMA
     hid, cache = pl.pallas_call(
         functools.partial(kernel, (S, B, heads, hd, micro, tok)),
@@ -311,24 +327,27 @@
             jax.ShapeDtypeStruct((rows, width), BF16),
             jax.ShapeDtypeStruct((2, rows, width), BF16),
         ),
-        in_specs=[smem] * 3 + [vmem] * 6,
+        in_specs=[smem] * 3 + [vmem, hbm, vmem, vmem, hbm, vmem],
         out_specs=(vmem, vmem),
         scratch_shapes=[
             pltpu.VMEM((B, rows, 2 * width), BF16),
+            pltpu.VMEM((2, heads, total, hd), BF16),
+            pltpu.VMEM((total, hd), BF16),
             pltpu.VMEM((B, rows, width), BF16),
             pltpu.VMEM((total, 2 * width), BF16),
+            pltpu.VMEM((text, 2 * width), BF16),
             pltpu.VMEM((text, 2 * width), BF16),
             pltpu.VMEM((3, B * depth, hd), BF16),
             pltpu.VMEM((2, B, rows, hd), BF16),
             pltpu.VMEM((text, hd), BF16),
             pltpu.VMEM((text, hd), BF16),
-            pltpu.VMEM((B, rows, hd), BF16),
+            pltpu.VMEM((total, hd), BF16),
             pltpu.VMEM((2, B, rows, hd), BF16),
             sem((B,)), sem((B,)), sem((B,)), sem((B,)),
             sem((heads,)), sem((B,)), sem((heads,)), sem((B,)),
             sem((B,)), sem((heads,)), sem((B,)), sem((heads,)),
             sem((B,)), sem((B,)), sem((B,)), sem((B,)), sem((B + 1,)),
-            sem((5,)),
+            sem((6,)),
         ],
         compiler_params=pltpu.CompilerParams(
             collective_id=0, has_side_effects=True, vmem_limit_bytes=60 * 1024 * 1024

time: 63.1 us -> 59.2 us (0.938); the launches traced: 62.1 us -> 59 us
  Pallas kernels: 58.7 us -> 55.6 us
    pallas_call x1, Pallas kernels: 58.7 us -> 55.6 us  [shards(): pl.pallas_call(functools.partial(kernel, (S, B, heads, hd, micro, tok)),...]
where the time goes in v3:
time: 59.2 us; the launch traced here: 59 us
  Pallas kernels  55.6 us (94%)
  local copies, waits for them, and re-layouts  2.1 us (4%)
  between operations  1.29 us (2%)
    pallas_call x1, Pallas kernels, shards(): pl.pallas_call(functools.partial(kernel, (S, B, heads, hd, micro, tok)),...  55.6 us
    unnamed x4, local copies, waits for them, and re-layouts  2.1 us

profile of v3, /device:TPU:7, one launch (start us, length us, event | category | flops | bytes accessed | tf_op | source)
XLA Modules:
  0.0 59.0 jit_solution(5155435650644947426)
XLA Ops:
  1.3 55.6 %shard_map.104 = (bf16[32,768]{1,0:T(8,128)(2,1)}, bf16[2,32,768]{2,1,0:T(8,128)(2,1)}) custom-call(s32[1]{0:T(128)S(6)} %copy.13.text_len, s32[4]{0:T(128)} %patch_len.1, s32[2,4]{1,0:T(2,128)} %bitcast.16, bf16[32,768]{1,0:T(8,128)(2,1)} %bitcast.15, bf16[3,192,768]{2,1,0:T(8,128)(2,1)} %bitcast.10, f32[1,1536]{1,0:T(1,128)} %row_gain.1, ...), custom_call_target="tpu_custom_call" | custom-call | tf_op jit(solution)/shard_map/pallas_call | solution.py:324
  56.9 0.0 copy-start
  56.9 1.5 %copy.14 = bf16[1,4,8,768]{3,2,1,0:T(8,128)(2,1)} copy(bf16[1,4,8,768]{3,2,1,0:T(8,128)(2,1)} %bitcast.14) | data formatting | bytes 98304
  58.3 0.0 copy-done
  58.3 0.6 %copy.15 = bf16[1,2,4,8,768]{4,3,2,1,0:T(8,128)(2,1)} copy(bf16[1,2,4,8,768]{4,3,2,1,0:T(8,128)(2,1)S(1)} %bitcast.13) | data formatting | bytes 196608
Async XLA Ops:
  56.9 1.5 %copy-start = (bf16[2,32,768]{2,1,0:T(8,128)(2,1)S(1)}, bf16[2,32,768]{2,1,0:T(8,128)(2,1)}, u32[]{:S(2)}) copy-start(bf16[2,32,768]{2,1,0:T(8,128)(2,1)} %get-tuple-element.5) | copy-start | bytes 294916
